TPU v7x, 512 devices: a whole 4x4x16 slice. The times are simulated.
512 devices in a mesh: seq: 32 (over z, core), head: 4 (over x), pool: 4 (over y).
Axes of the slice: x: 4, y: 4, z: 16, core: 2. Of those that a mesh axis runs over, the one named last changes fastest.
Arguments:
- tokens: bfloat16 [512, 4096], P(('seq', 'head'), 'pool'), may hold values from -6 to 6
- routes: int32 [512, 8], P(('seq', 'head')), may hold values from 0 to 31, all different within a row; in each aligned block of 4 rows (0 to 3, 4 to 7, ...) at most 2 rows name the same one
- gate_fixed: int32 [512, 8], P(('seq', 'head')), may hold values from 1 to 65535
- gate_weight: bfloat16 [32, 4096, 3072], P('seq', 'pool', 'head'), may hold values from -0.09375 to 0.09375
- up_weight: bfloat16 [32, 4096, 3072], P('seq', 'pool', 'head'), may hold values from -0.09375 to 0.09375
- down_weight: bfloat16 [32, 3072, 4096], P('seq', 'head', 'pool'), may hold values from -0.109375 to 0.109375
- gate_scale: bfloat16 [32, 32, 24], P('seq', 'pool', 'head'), may hold values from 0.5 to 2
- up_scale: bfloat16 [32, 32, 24], P('seq', 'pool', 'head'), may hold values from 0.5 to 2
- down_scale: bfloat16 [32, 24, 32], P('seq', 'head', 'pool'), may hold values from 0.5 to 2
Outputs:
- combined: bfloat16 [512, 4096], P(('seq', 'head'), 'pool')
Inputs may be any that keep to these rules, and one draw needn't show every extreme that they name: `routes`: each row names 8 different experts. Within the rows of one device (aligned blocks of 4 rows) no expert is named by more than 2 rows, and in some blocks one expert is named by exactly 2 rows.
All inputs are finite; a program needn't handle non-finite values.
Results may differ from a plain program's by a relative error of at most 0.02.
Values may be sent and summed in bfloat16 or wider, within the bound.
A program may use at most 64 MiB of HBM per device.

v0:
```python
import jax
import jax.numpy as jnp
from jax import lax
from jax.sharding import PartitionSpec as P

QB = 128
CAP = 2


largest_choice = lax.Precision.HIGHEST


def from_everyone(shard, axis):
    copies = jnp.broadcast_to(shard, (lax.axis_size(axis), *shard.shape))
    return lax.all_to_all(copies, axis, split_axis=0, concat_axis=0, tiled=True)


def laid_out(parts, dim):
    parts = jnp.moveaxis(parts, 0, dim)
    lengths = parts.shape
    return parts.reshape(*lengths[:dim], lengths[dim] * lengths[dim + 1], *lengths[dim + 2 :])


def collect(shard, axis, dim):
    parts = from_everyone(shard, axis)
    return laid_out(parts, dim)


def split_up(shard, dim, count):
    lengths = shard.shape
    parts = shard.reshape(*lengths[:dim], count, lengths[dim] // count, *lengths[dim + 1 :])
    return jnp.moveaxis(parts, dim, 0)


def sent_and_summed(shard, axis, dim):
    count = lax.axis_size(axis)
    parts = lax.all_to_all(split_up(shard, dim, count), axis, 0, 0, tiled=True)
    return jnp.sum(parts.astype(jnp.float32), axis=0)


def in_one_piece(arrays, axis, dim, along):
    both = jnp.concatenate(arrays, axis=along)
    filled, at, outs = (sent_and_summed(both, axis, dim), 0, [])
    for a in arrays:
        outs.append(lax.slice_in_dim(filled, at, at + a.shape[along], axis=along))
        at += a.shape[along]
    return tuple(outs)


def expand_scale(route_weight, scale):
    grown = jnp.repeat(jnp.repeat(scale, QB, axis=1), QB, axis=2)
    return route_weight * grown


def slot_positions(block_routes, expert_total):
    flattened = block_routes.reshape(-1)
    expert_ids = lax.broadcasted_iota(jnp.int32, (1, expert_total), 1)
    onehot = (flattened[:, None] == expert_ids).astype(jnp.int32)
    before = jnp.cumsum(onehot, axis=0) - onehot
    slot_index = jnp.sum(before * onehot, axis=1)
    return (flattened * CAP + slot_index).reshape(block_routes.shape)


def local_buffer(tokens, positions, slot_total):
    targets = lax.broadcasted_iota(jnp.int32, (slot_total, 1, 1), 0)
    selector = jnp.any(positions[None, :, :] == targets, axis=2).astype(jnp.bfloat16)
    return jnp.dot(selector, tokens, preferred_element_type=jnp.float32).astype(jnp.bfloat16)


def per_device(
    tokens,
    routes,
    gate_fixed,
    gate_weight,
    up_weight,
    down_weight,
    gate_scale,
    up_scale,
    down_scale,
):
    seq_count = lax.axis_size("seq")
    local_experts = gate_weight.shape[0]
    expert_total = local_experts * seq_count
    feature_width = tokens.shape[1]
    slot_total = expert_total * CAP
    gate_dense = expand_scale(gate_weight, gate_scale)
    up_dense = expand_scale(up_weight, up_scale)
    down_dense = expand_scale(down_weight, down_scale)
    positions = slot_positions(routes, expert_total)
    outgoing = local_buffer(tokens, positions, slot_total)
    outgoing = outgoing.reshape(seq_count, local_experts, 1, CAP, feature_width)
    arrived = lax.all_to_all(outgoing, "seq", split_axis=0, concat_axis=2, tiled=True)
    arrived = arrived.reshape(local_experts, seq_count, 1, CAP, feature_width)
    stacked_weight = jnp.concatenate([gate_dense, up_dense], axis=2)
    projected = jnp.einsum(
        "jshcd,jdf->jshcf",
        collect(arrived, "head", 2),
        stacked_weight,
        preferred_element_type=jnp.float32,
    )
    hidden_width = gate_dense.shape[2]
    gate_sum = projected[..., :hidden_width]
    up_sum = projected[..., hidden_width:]
    gate_share, up_share = in_one_piece(
        (gate_sum.astype(jnp.bfloat16), up_sum.astype(jnp.bfloat16)), "pool", 4, 0
    )
    hidden_share = (jax.nn.silu(gate_share) * up_share).astype(jnp.bfloat16)
    partial_out = jnp.einsum(
        "jshcf,jfd->jshcd",
        collect(hidden_share, "pool", 4),
        down_dense,
        preferred_element_type=jnp.float32,
    )
    summed = sent_and_summed(partial_out.astype(jnp.bfloat16), "head", 2)
    results_local = summed.astype(jnp.bfloat16).reshape(
        local_experts, seq_count, CAP, feature_width
    )
    results = lax.all_to_all(results_local, "seq", split_axis=1, concat_axis=0, tiled=True)
    results = results.reshape(slot_total, feature_width)
    fixed = gate_fixed.astype(jnp.float32)
    weights = fixed / jnp.sum(fixed, axis=1, keepdims=True)
    slot_ids = lax.broadcasted_iota(jnp.int32, (1, 1, slot_total), 2)
    combine_weight = jnp.sum(
        jnp.where(positions[:, :, None] == slot_ids, weights[:, :, None], 0.0), axis=1
    )
    combined = jnp.dot(
        combine_weight,
        results.astype(jnp.float32),
        precision=largest_choice,
        preferred_element_type=jnp.float32,
    )
    return combined.astype(jnp.bfloat16)


def solution(mesh):
    return jax.shard_map(
        per_device,
        mesh=mesh,
        in_specs=(
            P(("seq", "head"), "pool"),
            P(("seq", "head"), None),
            P(("seq", "head"), None),
            P("seq", "pool", "head"),
            P("seq", "pool", "head"),
            P("seq", "head", "pool"),
            P("seq", "pool", "head"),
            P("seq", "pool", "head"),
            P("seq", "head", "pool"),
        ),
        out_specs=P(("seq", "head"), "pool"),
        check_vma=False,
    )
```

profile of v0, /device:TPU:1, one launch (start us, length us, event | category | flops | bytes accessed | tf_op | source)
XLA Modules:
  0.0 122.6 jit_solution(3802836858634366784)
XLA Ops:
  0.0 0.8 eq.20
  1.2 0.7 multiply_add_fusion
  2.0 0.2 convolution_convert_fusion
  2.2 0.7 reshape.94
  2.9 16.7 %all-to-all-start = ((bf16[32,1,1,2,1024]{4,3,2,1,0:T(2,128)(2,1)}), bf16[32,1,1,2,1024]{4,3,2,1,0:T(2,128)(2,1)S(1)}, u32[]{:S(2)}, u32[]{:S(2)}) async-start(bf16[32,1,1,2,1024]{4,3,2,1,0:T(2,128)(2,1)} %bitcast), calls=%async_computation | async-start | bytes 262144 | tf_op jit(solution)/shard_map/all_to_all | solution.py:92
  19.7 0.8 copy.33
  20.4 15.1 %all-to-all-done = bf16[32,1,1,2,1024]{4,3,2,1,0:T(2,128)(2,1)S(1)} async-done(((bf16[32,1,1,2,1024]{4,3,2,1,0:T(2,128)(2,1)}), bf16[32,1,1,2,1024]{4,3,2,1,0:T(2,128)(2,1)S(1)}, u32[]{:S(2)}, u32[]{:S(2)}) %all-to-all-start) | async-done | bytes 131104 | tf_op jit(solution)/shard_map/all_to_all | solution.py:92
  35.5 0.9 broadcast_in_dim.52
  36.4 4.1 %all-to-all-start.1 = ((bf16[4,1,32,1,2,1024]{5,2,4,3,1,0:T(8,128)(2,1)}), bf16[4,1,32,1,2,1024]{5,2,4,3,1,0:T(8,128)(2,1)}, u32[]{:S(2)}, u32[]{:S(2)}) async-start(bf16[4,1,32,1,2,1024]{5,2,4,3,1,0:T(8,128)(2,1)} %broadcast_in_dim.52), calls=%async_computation.1 | async-start | bytes 1048576 | tf_op jit(solution)/shard_map/all_to_all | solution.py:15
  40.8 0.7 copy.34
  41.9 1.6 %copy.32 = bf16[1,1024,768]{2,1,0:T(8,128)(2,1)} copy(bf16[1,1024,768]{1,2,0:T(8,128)(2,1)S(1)} %bitcast.82) | data formatting | bytes 3145728 | tf_op jit(solution)/shard_map/broadcast_in_dim | solution.py:51
  43.5 2.0 %mul.33 = bf16[1,1024,768]{2,1,0:T(8,128)(2,1)S(1)} multiply(bf16[1,1024,768]{2,1,0:T(8,128)(2,1)} %param.13, bf16[1,1024,768]{2,1,0:T(8,128)(2,1)S(1)} %copy.34) | non-fusion elementwise | flops 786432 | bytes 4718592 | tf_op jit(solution)/shard_map/mul | solution.py:52
  45.6 0.3 copy-done.2
  45.9 0.4 mul.32
  46.3 1.8 %all-to-all-done.1 = bf16[4,1,32,1,2,1024]{5,2,4,3,1,0:T(8,128)(2,1)} async-done(((bf16[4,1,32,1,2,1024]{5,2,4,3,1,0:T(8,128)(2,1)}), bf16[4,1,32,1,2,1024]{5,2,4,3,1,0:T(8,128)(2,1)}, u32[]{:S(2)}, u32[]{:S(2)}) %all-to-all-start.1) | async-done | bytes 524320 | tf_op jit(solution)/shard_map/all_to_all | solution.py:15
  48.1 2.0 %fusion.4 = bf16[1,32,4,2,1536]{4,1,3,2,0:T(8,128)(2,1)S(1)} fusion(bf16[1,1024,768]{2,1,0:T(8,128)(2,1)S(1)} %mul.33, bf16[1,1024,768]{2,1,0:T(8,128)(2,1)S(1)} %mul.32, bf16[4,1,32,1,2,1024]{5,2,4,3,1,0:T(8,128)(2,1)} %all-to-all-done.1), kind=kOutput, calls=%fused_computation.5 | convolution fusion | flops 811991040 | bytes 4456448 | tf_op jit(solution)/shard_map/jshcd,jdf->jshcf/dot_general | solution.py:95
  50.3 0.9 reshape.98
  51.4 16.0 %all_to_all.38 = bf16[4,2,32,4,2,192]{5,2,4,3,1,0:T(8,128)(2,1)S(1)} all-to-all(bf16[4,2,32,4,2,192]{5,2,4,3,1,0:T(8,128)(2,1)S(1)} %bitcast.83), channel_id=1, replica_groups=mesh['seq'=32,'head'=4,'pool'=4] {'pool'}, dimensions={0} | all-to-all | bytes 1572864 | tf_op jit(solution)/shard_map/all_to_all | solution.py:37
  67.4 0.2 convert_reduce_fusion
  67.7 0.9 broadcast_in_dim.61
  68.6 4.1 %all-to-all-start.3 = ((bf16[4,1,32,4,2,192]{5,2,4,3,1,0:T(8,128)(2,1)}), bf16[4,1,32,4,2,192]{5,2,4,3,1,0:T(8,128)(2,1)}, u32[]{:S(2)}, u32[]{:S(2)}) async-start(bf16[4,1,32,4,2,192]{5,2,4,3,1,0:T(8,128)(2,1)} %broadcast_in_dim.61), calls=%async_computation.3 | async-start | bytes 1048576 | tf_op jit(solution)/shard_map/all_to_all | solution.py:15
  72.7 1.0 broadcast_in_dim.64
  73.7 0.7 broadcast_in_dim.65
  74.5 5.2 %all-to-all-done.3 = bf16[4,1,32,4,2,192]{5,2,4,3,1,0:T(8,128)(2,1)} async-done(((bf16[4,1,32,4,2,192]{5,2,4,3,1,0:T(8,128)(2,1)}), bf16[4,1,32,4,2,192]{5,2,4,3,1,0:T(8,128)(2,1)}, u32[]{:S(2)}, u32[]{:S(2)}) %all-to-all-start.3) | async-done | bytes 393248 | tf_op jit(solution)/shard_map/all_to_all | solution.py:15
  79.7 1.5 %copy.36 = bf16[1,32,4,2,4,192]{5,4,1,3,2,0:T(4,128)(2,1)S(1)} copy(bf16[1,32,4,2,4,192]{5,1,3,2,0,4:T(8,128)(2,1)} %bitcast.15) | data formatting | bytes 786432 | tf_op jit(solution)/shard_map/transpose | solution.py:19
  81.1 0.5 reshape.99
  81.6 2.1 %fusion.11 = bf16[4,1,32,1,2,1024]{5,2,4,3,1,0:T(8,128)(2,1)S(1)} fusion(bf16[32,4,2,768]{3,0,2,1:T(8,128)(2,1)S(1)} %reshape.99, bf16[1,768,1024]{2,1,0:T(8,128)(2,1)} %param.14, bf16[1,768,1024]{2,1,0:T(8,128)(2,1)S(1)} %broadcast_in_dim.65), kind=kOutput, calls=%fused_computation.11 | convolution fusion | flops 403701760 | bytes 4063232 | tf_op jit(solution)/shard_map/jshcf,jfd->jshcd/dot_general | solution.py:108
  83.7 9.9 %all_to_all.39 = bf16[4,1,32,1,2,1024]{5,2,4,3,1,0:T(8,128)(2,1)S(1)} all-to-all(bf16[4,1,32,1,2,1024]{5,2,4,3,1,0:T(8,128)(2,1)S(1)} %fusion.11), channel_id=1, replica_groups=mesh['seq'=32,'head'=4,'pool'=4] {'head'}, dimensions={0} | all-to-all | bytes 1048576 | tf_op jit(solution)/shard_map/all_to_all | solution.py:37
  93.7 0.8 copy.39
  94.4 11.5 %all-to-all-start.5 = ((bf16[1,32,2,1024]{3,2,0,1:T(2,128)(2,1)}), bf16[1,32,2,1024]{3,2,0,1:T(2,128)(2,1)S(1)}, u32[]{:S(2)}, u32[]{:S(2)}) async-start(bf16[1,32,2,1024]{3,2,0,1:T(2,128)(2,1)} %copy.39), calls=%async_computation.5 | async-start | bytes 262144 | tf_op jit(solution)/shard_map/all_to_all | solution.py:118
  106.2 15.6 %all-to-all-done.5 = bf16[1,32,2,1024]{3,2,0,1:T(2,128)(2,1)S(1)} async-done(((bf16[1,32,2,1024]{3,2,0,1:T(2,128)(2,1)}), bf16[1,32,2,1024]{3,2,0,1:T(2,128)(2,1)S(1)}, u32[]{:S(2)}, u32[]{:S(2)}) %all-to-all-start.5) | async-done | bytes 131104 | tf_op jit(solution)/shard_map/all_to_all | solution.py:118
  121.8 0.8 convolution_convert_fusion.1
  (34 shorter events, 2.0 us)
Async XLA Ops:
  0.0 2.0 %copy-start = (bf16[4,1024]{1,0:T(4,128)(2,1)S(1)}, bf16[4,1024]{1,0:T(4,128)(2,1)}, u32[]{:S(2)}) copy-start(bf16[4,1024]{1,0:T(4,128)(2,1)} %param.9) | copy-start | bytes 24580
  2.9 32.6 %all-to-all-start = ((bf16[32,1,1,2,1024]{4,3,2,1,0:T(2,128)(2,1)}), bf16[32,1,1,2,1024]{4,3,2,1,0:T(2,128)(2,1)S(1)}, u32[]{:S(2)}, u32[]{:S(2)}) async-start(bf16[32,1,1,2,1024]{4,3,2,1,0:T(2,128)(2,1)} %bitcast), calls=%async_computation | async-start | bytes 262144 | tf_op jit(solution)/shard_map/all_to_all | solution.py:92
  36.4 11.7 %all-to-all-start.1 = ((bf16[4,1,32,1,2,1024]{5,2,4,3,1,0:T(8,128)(2,1)}), bf16[4,1,32,1,2,1024]{5,2,4,3,1,0:T(8,128)(2,1)}, u32[]{:S(2)}, u32[]{:S(2)}) async-start(bf16[4,1,32,1,2,1024]{5,2,4,3,1,0:T(8,128)(2,1)} %broadcast_in_dim.52), calls=%async_computation.1 | async-start | bytes 1048576 | tf_op jit(solution)/shard_map/all_to_all | solution.py:15
  40.8 0.7 copy-start.5
  43.5 2.0 %copy-start.1 = (bf16[1,1024,768]{2,1,0:T(8,128)(2,1)S(1)}, bf16[1,1024,768]{2,1,0:T(8,128)(2,1)}, u32[]{:S(2)}) copy-start(bf16[1,1024,768]{2,1,0:T(8,128)(2,1)} %copy.32) | copy-start | bytes 4718596
  43.5 2.4 %copy-start.2 = (bf16[1,1024,768]{2,1,0:T(8,128)(2,1)S(1)}, bf16[1,1024,768]{2,1,0:T(8,128)(2,1)}, u32[]{:S(2)}) copy-start(bf16[1,1024,768]{2,1,0:T(8,128)(2,1)} %param.12) | copy-start | bytes 4718596
  67.6 5.1 %copy-start.4 = (bf16[1,6,8]{2,1,0:T(8,128)(2,1)S(1)}, bf16[1,6,8]{2,1,0:T(8,128)(2,1)}, u32[]{:S(2)}) copy-start(bf16[1,6,8]{2,1,0:T(8,128)(2,1)} %param.17) | copy-start | bytes 292
  68.6 11.1 %all-to-all-start.3 = ((bf16[4,1,32,4,2,192]{5,2,4,3,1,0:T(8,128)(2,1)}), bf16[4,1,32,4,2,192]{5,2,4,3,1,0:T(8,128)(2,1)}, u32[]{:S(2)}, u32[]{:S(2)}) async-start(bf16[4,1,32,4,2,192]{5,2,4,3,1,0:T(8,128)(2,1)} %broadcast_in_dim.61), calls=%async_computation.3 | async-start | bytes 1048576 | tf_op jit(solution)/shard_map/all_to_all | solution.py:15
  83.7 22.2 %copy-start.3 = (s32[4,8]{1,0:T(4,128)S(1)}, s32[4,8]{1,0:T(4,128)}, u32[]{:S(2)}) copy-start(s32[4,8]{1,0:T(4,128)} %param.11) | copy-start | bytes 388
  94.4 27.3 %all-to-all-start.5 = ((bf16[1,32,2,1024]{3,2,0,1:T(2,128)(2,1)}), bf16[1,32,2,1024]{3,2,0,1:T(2,128)(2,1)S(1)}, u32[]{:S(2)}, u32[]{:S(2)}) async-start(bf16[1,32,2,1024]{3,2,0,1:T(2,128)(2,1)} %copy.39), calls=%async_computation.5 | async-start | bytes 262144 | tf_op jit(solution)/shard_map/all_to_all | solution.py:118
where the time goes:
time: 123 us
  waiting for transfers between devices  37.7 us (31%)
  starting transfers between devices  36.5 us (30%)
  blocking collectives  25.9 us (21%)
  local copies, waits for them, and re-layouts  13 us (11%)
  matrix products  5.12 us (4%)
  other arithmetic  4.22 us (3%)
    all_to_all x2, blocking collectives, sent_and_summed(): parts = lax.all_to_all(split_up(shard, dim, count), axis, 0, 0, tiled=True)  25.9 us
    all_to_all x1, starting transfers between devices, per_device(): lax.all_to_all(outgoing, 'seq', split_axis=0, concat_axis=2, tiled=True)  16.7 us
    all_to_all x1, waiting for transfers between devices, per_device(): lax.all_to_all(results_local, 'seq', split_axis=1, concat_axis=0, tiled=T...  15.6 us
    all_to_all x1, waiting for transfers between devices, per_device(): lax.all_to_all(outgoing, 'seq', split_axis=0, concat_axis=2, tiled=True)  15.1 us
    all_to_all x1, starting transfers between devices, per_device(): lax.all_to_all(results_local, 'seq', split_axis=1, concat_axis=0, tiled=T...  11.5 us
    all_to_all x2, starting transfers between devices, from_everyone(): return lax.all_to_all(copies, axis, split_axis=0, concat_axis=0, tiled=True)  8.26 us
    all_to_all x2, waiting for transfers between devices, from_everyone(): return lax.all_to_all(copies, axis, split_axis=0, concat_axis=0, tiled=True)  7.06 us
    broadcast_in_dim x7, local copies, waits for them, and re-layouts, expand_scale(): grown = jnp.repeat(jnp.repeat(scale, QB, axis=1), QB, axis=2)  4.41 us
  transfers between devices with their start and end apart: 4, of which 4 were waited for; matrix products, arithmetic and copies ran while one was open for 7% of the time, Pallas kernels for 0%

commit v1 on v0

v1 whole, which is shorter than its diff:
```python
import functools

import jax
import jax.numpy as jnp
from jax import lax
from jax.experimental import pallas as pl
from jax.experimental.pallas import tpu as pltpu
from jax.sharding import PartitionSpec as P

QB = 128
CAP = 2
NX = 4
CHUNKS = 4
F32 = jnp.float32
BF16 = jnp.bfloat16


def offset(i):
    k = (i + 1) // 2
    return k if i % 2 == 0 else -k


def opposite(i, nz):
    if i == 0:
        return 0
    other = i + 1 if i % 2 else i - 1
    return other if other < nz else i


class Copies:
    def __init__(self):
        self.sent = []

    def make(self, src, dst, send, recv, device):
        return pltpu.make_async_remote_copy(
            src_ref=src,
            dst_ref=dst,
            send_sem=send,
            recv_sem=recv,
            device_id=device,
            device_id_type=pl.DeviceIdType.MESH,
        )

    def start(self, *args):
        copy = self.make(*args)
        copy.start()
        self.sent.append(copy)


def kernel(
    nz,
    tokens_hbm,
    routes_hbm,
    fixed_hbm,
    gate_hbm,
    up_hbm,
    down_hbm,
    gs_hbm,
    us_hbm,
    ds_hbm,
    out_ref,
    tokens,
    routes,
    fixed,
    w1,
    w2,
    gs,
    us,
    ds_,
    grown1,
    grown2,
    slots,
    gathered,
    wide,
    x_ref,
    partial,
    relay_y,
    sums_y,
    arrive_y,
    hidden,
    outs,
    relay_x,
    sums_x,
    arrive_x,
    back_wide,
    back,
    results,
    load_sem,
    zs,
    zr,
    gx_s,
    gx_r,
    ry_s,
    ry_r,
    gy_s,
    gy_r,
    rx_s,
    rx_r,
    bs,
    br,
):
    s = lax.axis_index("seq")
    h = lax.axis_index("head")
    p = lax.axis_index("pool")
    z = s // 2
    core = s % 2
    nc = CHUNKS
    ni = nz // nc
    ne = 2 * nz
    m = NX * ni * 2 * CAP
    share = m // NX
    f1 = w1.shape[1] // 2
    dw = w2.shape[1]
    jw = dw // 128

    def near(base, step):
        return (base + step + NX) % NX

    xr, xl, xo = near(h, 1), near(h, -1), near(h, 2)
    yr, yl, yo = near(p, 1), near(p, -1), near(p, 2)
    dev_xr, dev_xl = (s, xr, p), (s, xl, p)
    dev_yr, dev_yl = (s, h, yr), (s, h, yl)

    def chip(i, to_core):
        return (((z + offset(i) + nz) % nz) * 2 + to_core, h, p)

    peers = [(i, c) for i in range(nz) for c in (0, 1)]

    barrier = pltpu.get_barrier_semaphore()
    for i in range(nz - 1, 0, -1):
        for c in (0, 1):
            pl.semaphore_signal(barrier, inc=1, device_id=chip(i, c), device_id_type=pl.DeviceIdType.MESH)
    for dev in (chip(0, 1 - core), dev_xr, dev_xl, dev_yr, dev_yl):
        pl.semaphore_signal(barrier, inc=1, device_id=dev, device_id_type=pl.DeviceIdType.MESH)

    loads = [
        (tokens_hbm, tokens),
        (routes_hbm, routes),
        (fixed_hbm, fixed),
        (gs_hbm, gs),
        (us_hbm, us),
        (ds_hbm, ds_),
        (gate_hbm.at[0], w1.at[:, pl.ds(0, f1)]),
        (up_hbm.at[0], w1.at[:, pl.ds(f1, f1)]),
        (down_hbm.at[0], w2),
    ]
    loads = [pltpu.make_async_copy(a, b, load_sem.at[n]) for n, (a, b) in enumerate(loads)]
    for load in loads:
        load.start()
    for load in loads[:3]:
        load.wait()

    lane = lax.broadcasted_iota(jnp.int32, (4, 128), 1)
    ids = routes[...]
    gates = fixed[...].astype(F32)
    weights = gates / jnp.sum(gates, axis=1, keepdims=True)
    names = jnp.zeros((4, 128), F32)
    weight = jnp.zeros((4, 128), F32)
    for k in range(ids.shape[1]):
        hit = ids[:, k : k + 1] == lane // CAP
        names = names + jnp.where(hit, 1.0, 0.0)
        weight = weight + jnp.where(hit, weights[:, k : k + 1], 0.0)
    before = [jnp.zeros((1, 128), F32)]
    for r in range(3):
        before.append(before[-1] + names[r : r + 1])
    before = jnp.concatenate(before, axis=0)
    selected = (names > 0.5) & (before == (lane % CAP).astype(F32))
    pick = jnp.where(selected, 1.0, 0.0)
    combine = jnp.where(selected, weight, 0.0)
    pick = jnp.concatenate([pick, jnp.zeros((4, 128), F32)], axis=0)
    pick = pick.T.astype(BF16)
    rows = tokens[...].astype(F32)
    rows = jnp.concatenate([rows, jnp.zeros_like(rows)], axis=0).astype(BF16)
    for j in range(jw):
        part = jnp.dot(pick, rows[:, j * 128 : (j + 1) * 128], preferred_element_type=F32)
        wide[pl.ds(j, ne * CAP, stride=jw), :] = part[: ne * CAP]
    for e in range(0, ne, 8):
        slots[e : e + 8] = wide[e * 16 : (e + 8) * 16, :].reshape(8, 16, 128).astype(BF16)

    c = Copies()
    pl.semaphore_wait(barrier, 2 * (nz - 1) + 5)

    gathered[h, 0, core] = slots[s]
    c.start(slots.at[z * 2 + 1 - core], gathered.at[h, 0, core], zs.at[1 - core], zr.at[core], chip(0, 1 - core))
    for i in range(1, nz):
        there = opposite(i, nz)
        for to in (0, 1):
            dev = chip(i, to)
            c.start(
                slots.at[dev[0]],
                gathered.at[h, there, core],
                zs.at[i * 2 + to],
                zr.at[there * 2 + core],
                dev,
            )

    for load in loads[3:]:
        load.wait()

    def grow(scale, count):
        v = scale[0].astype(F32)
        return jnp.concatenate(
            [jnp.broadcast_to(v[:, j : j + 1], (v.shape[0], 128)) for j in range(count)], axis=1
        )

    grown1[:, :f1] = grow(gs, f1 // QB)
    grown1[:, f1:] = grow(us, f1 // QB)
    grown2[...] = grow(ds_, dw // QB)

    def scale_w1(n, _):
        at = pl.ds(pl.multiple_of(n * 32, 32), 32)
        by = grown1[pl.ds(n // 4, 1), :]
        for half in (0, 1):
            cols = slice(half * f1, (half + 1) * f1)
            w1[at, cols] = (w1[at, cols].astype(F32) * by[:, cols]).astype(BF16)
        return 0

    def scale_w2(n, _):
        at = pl.ds(pl.multiple_of(n * 32, 32), 32)
        w2[at, :] = (w2[at, :].astype(F32) * grown2[pl.ds(n // 4, 1), :]).astype(BF16)
        return 0

    lax.fori_loop(0, w1.shape[0] // 32, scale_w1, 0)
    lax.fori_loop(0, w2.shape[0] // 32, scale_w2, 0)

    def span(k, part=None):
        if part is None:
            return pl.ds(k * ni, ni)
        return pl.ds(k * ni + part * (ni // 2), ni // 2)

    def recv(dst, sem, send=None):
        c.make(dst, dst, zs.at[0] if send is None else send, sem, dev_xr).wait_recv()

    def stage0(k):
        for i in range(k * ni, (k + 1) * ni):
            for frm in (0, 1):
                if i == 0:
                    continue
                recv(gathered.at[h, i, frm], zr.at[i * 2 + frm])
        if k == 0:
            recv(gathered.at[h, 0, 1 - core], zr.at[1 - core])
        block = gathered.at[h, span(k)]
        c.start(block, block, gx_s.at[k, 0], gx_r.at[k, 0], dev_xr)
        c.start(block, block, gx_s.at[k, 1], gx_r.at[k, 1], dev_xl)

    def stage1(k):
        recv(gathered.at[xl, span(k)], gx_r.at[k, 0])
        block = gathered.at[xl, span(k, 1)]
        c.start(block, block, gx_s.at[k, 2], gx_r.at[k, 2], dev_xr)
        recv(gathered.at[xr, span(k)], gx_r.at[k, 1])
        block = gathered.at[xr, span(k, 0)]
        c.start(block, block, gx_s.at[k, 3], gx_r.at[k, 3], dev_xl)

    def stage2(k):
        recv(gathered.at[xo, span(k, 1)], gx_r.at[k, 2])
        recv(gathered.at[xo, span(k, 0)], gx_r.at[k, 3])
        per = ni * 2 * 16
        for a in range(NX):
            wide[a * per : (a + 1) * per, :] = (
                gathered[a, k * ni : (k + 1) * ni].astype(F32).reshape(per, 128)
            )
        for j in range(jw):
            x_ref[:, j * 128 : (j + 1) * 128] = wide[pl.ds(j, m, stride=jw), :].astype(BF16)
        tiles = f1 // 256

        def tile(n, _):
            cols = pl.ds(pl.multiple_of(n * 256, 256), 256)
            part = jnp.dot(x_ref[...], w1[:, cols], preferred_element_type=F32)
            at = pl.ds(pl.multiple_of((n % tiles) * 256, 256), 256)
            partial[k, n // tiles, :, :, at] = part.reshape(NX, share, 256).astype(BF16)
            return 0

        lax.fori_loop(0, 2 * tiles, tile, 0)
        c.start(partial.at[k, 0, yo], relay_y.at[k, 0], ry_s.at[k, 0], ry_r.at[k, 0], dev_yr)
        c.start(partial.at[k, 1, yo], relay_y.at[k, 1], ry_s.at[k, 1], ry_r.at[k, 1], dev_yl)
        c.start(partial.at[k, 1, yr], arrive_y.at[k, 0, 1], ry_s.at[k, 2], ry_r.at[k, 2], dev_yr)
        c.start(partial.at[k, 0, yl], arrive_y.at[k, 1, 0], ry_s.at[k, 3], ry_r.at[k, 3], dev_yl)

    def stage3(k):
        recv(relay_y.at[k, 0], ry_r.at[k, 0])
        sums_y[k, 0] = (partial[k, 0, yr].astype(F32) + relay_y[k, 0].astype(F32)).astype(BF16)
        c.start(sums_y.at[k, 0], arrive_y.at[k, 0, 0], ry_s.at[k, 4], ry_r.at[k, 4], dev_yr)
        recv(relay_y.at[k, 1], ry_r.at[k, 1])
        sums_y[k, 1] = (partial[k, 1, yl].astype(F32) + relay_y[k, 1].astype(F32)).astype(BF16)
        c.start(sums_y.at[k, 1], arrive_y.at[k, 1, 1], ry_s.at[k, 5], ry_r.at[k, 5], dev_yl)

    def stage4(k):
        recv(arrive_y.at[k, 0, 1], ry_r.at[k, 2])
        recv(arrive_y.at[k, 1, 0], ry_r.at[k, 3])
        recv(arrive_y.at[k, 0, 0], ry_r.at[k, 4])
        recv(arrive_y.at[k, 1, 1], ry_r.at[k, 5])
        g, u = [
            partial[k, n, p].astype(F32) + arrive_y[k, 0, n].astype(F32) + arrive_y[k, 1, n].astype(F32)
            for n in (0, 1)
        ]
        hidden[k, p] = (g / (1.0 + jnp.exp(-g)) * u).astype(BF16)
        block = hidden.at[k, p]
        c.start(block, block, gy_s.at[k, 0], gy_r.at[k, 0], dev_yr)
        c.start(block, block, gy_s.at[k, 1], gy_r.at[k, 1], dev_yl)

    left, right = pl.ds(0, f1 // 2), pl.ds(f1 // 2, f1 // 2)

    def stage5(k):
        recv(hidden.at[k, yl], gy_r.at[k, 0])
        block = hidden.at[k, yl, :, left]
        c.start(block, block, gy_s.at[k, 2], gy_r.at[k, 2], dev_yr)
        recv(hidden.at[k, yr], gy_r.at[k, 1])
        block = hidden.at[k, yr, :, right]
        c.start(block, block, gy_s.at[k, 3], gy_r.at[k, 3], dev_yl)

    def stage6(k):
        recv(hidden.at[k, yo, :, left], gy_r.at[k, 2])
        recv(hidden.at[k, yo, :, right], gy_r.at[k, 3])
        tiles = dw // 512

        def tile(n, _):
            cols = pl.ds(pl.multiple_of(n * 256, 256), 256)
            act = hidden[k].reshape(m, f1)
            part = jnp.dot(act, w2[:, cols], preferred_element_type=F32)
            at = pl.ds(pl.multiple_of((n % tiles) * 256, 256), 256)
            outs[k, n // tiles, :, :, at] = part.reshape(NX, share, 256).astype(BF16)
            return 0

        lax.fori_loop(0, 2 * tiles, tile, 0)
        c.start(outs.at[k, 0, xo], relay_x.at[k, 0], rx_s.at[k, 0], rx_r.at[k, 0], dev_xr)
        c.start(outs.at[k, 1, xo], relay_x.at[k, 1], rx_s.at[k, 1], rx_r.at[k, 1], dev_xl)
        c.start(outs.at[k, 1, xr], arrive_x.at[k, 0, 1], rx_s.at[k, 2], rx_r.at[k, 2], dev_xr)
        c.start(outs.at[k, 0, xl], arrive_x.at[k, 1, 0], rx_s.at[k, 3], rx_r.at[k, 3], dev_xl)

    def stage7(k):
        recv(relay_x.at[k, 0], rx_r.at[k, 0])
        sums_x[k, 0] = (outs[k, 0, xr].astype(F32) + relay_x[k, 0].astype(F32)).astype(BF16)
        c.start(sums_x.at[k, 0], arrive_x.at[k, 0, 0], rx_s.at[k, 4], rx_r.at[k, 4], dev_xr)
        recv(relay_x.at[k, 1], rx_r.at[k, 1])
        sums_x[k, 1] = (outs[k, 1, xl].astype(F32) + relay_x[k, 1].astype(F32)).astype(BF16)
        c.start(sums_x.at[k, 1], arrive_x.at[k, 1, 1], rx_s.at[k, 5], rx_r.at[k, 5], dev_xl)

    def stage8(k):
        recv(arrive_x.at[k, 0, 1], rx_r.at[k, 2])
        recv(arrive_x.at[k, 1, 0], rx_r.at[k, 3])
        recv(arrive_x.at[k, 0, 0], rx_r.at[k, 4])
        recv(arrive_x.at[k, 1, 1], rx_r.at[k, 5])
        for n in (0, 1):
            y = outs[k, n, h].astype(F32) + arrive_x[k, 0, n].astype(F32) + arrive_x[k, 1, n].astype(F32)
            for j in range(jw // 2):
                back_wide[pl.ds(n * (jw // 2) + j, share, stride=jw), :] = y[:, j * 128 : (j + 1) * 128]
        back[k] = back_wide[...].reshape(ni, 2, 16, 128).astype(BF16)
        for n in reversed(range(ni)):
            i = k * ni + n
            for to in (0, 1):
                if i == 0:
                    continue
                there = opposite(i, nz)
                c.start(
                    back.at[k, n, to], results.at[s], bs.at[i * 2 + to], br.at[there * 2 + core], chip(i, to)
                )
        if k == 0:
            c.start(back.at[0, 0, 1 - core], results.at[s], bs.at[1 - core], br.at[core], chip(0, 1 - core))
            results[s] = back[0, 0, core]

    stages = [stage0, stage1, stage2, stage3, stage4, stage5, stage6, stage7, stage8]
    for t in range(len(stages) + nc - 1):
        for k in range(nc):
            if 0 <= t - k < len(stages):
                stages[t - k](k)

    for i, frm in peers:
        if i == 0:
            continue
        recv(results.at[chip(i, frm)[0]], br.at[i * 2 + frm])
    recv(results.at[z * 2 + 1 - core], br.at[1 - core])

    high = combine.astype(BF16).astype(F32)
    both = jnp.concatenate([high, combine - high], axis=0)[:, : ne * CAP].astype(BF16)
    for e in range(0, ne, 8):
        wide[e * 16 : (e + 8) * 16, :] = results[e : e + 8].astype(F32).reshape(128, 128)
    for j in range(jw):
        got = wide[pl.ds(j, ne * CAP, stride=jw), :].astype(BF16)
        part = jnp.dot(both, got, preferred_element_type=F32)
        out_ref[:, j * 128 : (j + 1) * 128] = (part[:4] + part[4:]).astype(BF16)
    for copy in c.sent:
        copy.wait_send()


def solution(mesh):
    nz = mesh.shape["seq"] // 2

    def step(*args):
        tokens, routes, fixed, gate, _, down, gs, us, ds_ = args
        dw, f1 = gate.shape[1:]
        nc, ni = CHUNKS, nz // CHUNKS
        m = NX * ni * 2 * CAP
        share = m // NX
        ne = 2 * nz
        dma = pltpu.SemaphoreType.DMA
        scratch = [
            pltpu.VMEM(tokens.shape, BF16),
            pltpu.VMEM(routes.shape, jnp.int32),
            pltpu.VMEM(fixed.shape, jnp.int32),
            pltpu.VMEM((dw, 2 * f1), BF16),
            pltpu.VMEM((f1, dw), BF16),
            pltpu.VMEM(gs.shape, BF16),
            pltpu.VMEM(us.shape, BF16),
            pltpu.VMEM(ds_.shape, BF16),
            pltpu.VMEM((dw // QB, 2 * f1), F32),
            pltpu.VMEM((f1 // QB, dw), F32),
            pltpu.VMEM((ne, 16, 128), BF16),
            pltpu.VMEM((NX, nz, 2, 16, 128), BF16),
            pltpu.VMEM((max(m, ne * CAP) * 8, 128), F32),
            pltpu.VMEM((m, dw), BF16),
            pltpu.VMEM((nc, 2, NX, share, f1), BF16),
            pltpu.VMEM((nc, 2, share, f1), BF16),
            pltpu.VMEM((nc, 2, share, f1), BF16),
            pltpu.VMEM((nc, 2, 2, share, f1), BF16),
            pltpu.VMEM((nc, NX, share, f1), BF16),
            pltpu.VMEM((nc, 2, NX, share, dw // 2), BF16),
            pltpu.VMEM((nc, 2, share, dw // 2), BF16),
            pltpu.VMEM((nc, 2, share, dw // 2), BF16),
            pltpu.VMEM((nc, 2, 2, share, dw // 2), BF16),
            pltpu.VMEM((share * 8, 128), F32),
            pltpu.VMEM((nc, ni, 2, 16, 128), BF16),
            pltpu.VMEM((ne, 16, 128), BF16),
            dma((9,)),
            dma((2 * nz,)),
            dma((2 * nz,)),
            dma((nc, 4)),
            dma((nc, 4)),
            dma((nc, 6)),
            dma((nc, 6)),
            dma((nc, 4)),
            dma((nc, 4)),
            dma((nc, 6)),
            dma((nc, 6)),
            dma((2 * nz,)),
            dma((2 * nz,)),
        ]
        return pl.pallas_call(
            functools.partial(kernel, nz),
            out_shape=jax.ShapeDtypeStruct(tokens.shape, BF16),
            in_specs=[pl.BlockSpec(memory_space=pl.ANY)] * 9,
            out_specs=pl.BlockSpec(memory_space=pltpu.VMEM),
            scratch_shapes=scratch,
            compiler_params=pltpu.CompilerParams(
                collective_id=0, has_side_effects=True, vmem_limit_bytes=40 * 1024 * 1024
            ),
        )(*args)

    return jax.shard_map(
        step,
        mesh=mesh,
        in_specs=(
            P(("seq", "head"), "pool"),
            P(("seq", "head"), None),
            P(("seq", "head"), None),
            P("seq", "pool", "head"),
            P("seq", "pool", "head"),
            P("seq", "head", "pool"),
            P("seq", "pool", "head"),
            P("seq", "pool", "head"),
            P("seq", "head", "pool"),
        ),
        out_specs=P(("seq", "head"), "pool"),
        check_vma=False,
    )
```

time: 123 us -> 85.2 us (0.69)
  Pallas kernels: 0 us -> 75.9 us
  waiting for transfers between devices: 37.7 us -> 0 us
  starting transfers between devices: 36.5 us -> 0 us
  blocking collectives: 25.9 us -> 0 us
  matrix products: 5.12 us -> 0 us
  other arithmetic: 4.22 us -> 0 us
  local copies, waits for them, and re-layouts: 13 us -> 8.92 us
    pallas_call x0 -> x1, Pallas kernels: none -> 75.9 us  [step(): pl.pallas_call(functools.partial(kernel, nz), out_shape=jax.ShapeDtypeStr...]
    all_to_all x4 -> x0, waiting for transfers between devices: 37.7 us -> none  [the longest x1 15.6 us: per_device(): lax.all_to_all(results_local, 'seq', split_axis=1, concat_axis=0, tiled=T...]
    all_to_all x4 -> x0, starting transfers between devices: 36.5 us -> none  [the longest x1 16.7 us: per_device(): lax.all_to_all(outgoing, 'seq', split_axis=0, concat_axis=2, tiled=True)]
    all_to_all x2 -> x0, blocking collectives: 25.9 us -> none  [sent_and_summed(): parts = lax.all_to_all(split_up(shard, dim, count), axis, 0, 0, tiled=True)]
    unnamed x16 -> x19, local copies, waits for them, and re-layouts: 0.51 us -> 8.92 us
    broadcast_in_dim x9 -> x0, local copies, waits for them, and re-layouts: 6.14 us -> none  [the longest x7 4.41 us: expand_scale(): grown = jnp.repeat(jnp.repeat(scale, QB, axis=1), QB, axis=2)]
    dot_general x4 -> x0, matrix products: 5.12 us -> none  [the longest x1 2.07 us: per_device(): jnp.einsum('jshcf,jfd->jshcd', collect(hidden_share, 'pool', 4), down_den...]
    reshape x6 -> x0, local copies, waits for them, and re-layouts: 2.62 us -> none  [the longest x2 1.08 us: split_up(): shard.reshape(*lengths[:dim], count, lengths[dim] // count, *lengths[dim...]
  transfers between devices with their start and end apart: 4 -> 0, of which waited for: 4 -> 0; matrix products, arithmetic and copies ran while one was open for 7% -> 0% of each run, Pallas kernels for 0% -> 0%
where the time goes in v1:
time: 85.2 us; the launch traced here: 84.8 us
  Pallas kernels  75.9 us (89%)
  local copies, waits for them, and re-layouts  8.92 us (10%)
    pallas_call x1, Pallas kernels, step(): pl.pallas_call(functools.partial(kernel, nz), out_shape=jax.ShapeDtypeStr...  75.9 us
    unnamed x19, local copies, waits for them, and re-layouts  8.92 us

profile of v1, /device:TPU:1, one launch (start us, length us, event | category | flops | bytes accessed | tf_op | source)
XLA Modules:
  0.0 84.8 jit_solution(12019048770346558399)
XLA Ops:
  0.0 0.0 copy-start
  0.0 1.4 %copy-done = bf16[1,1024,768]{2,1,0:T(8,128)(2,1)S(1)} copy-done((bf16[1,1024,768]{2,1,0:T(8,128)(2,1)S(1)}, bf16[1,1024,768]{2,1,0:T(8,128)(2,1)}, u32[]{:S(2)}) %copy-start) | copy-done | bytes 1572888
  1.4 0.0 copy-start.1
  1.4 1.4 %copy-done.1 = bf16[1,1024,768]{2,1,0:T(8,128)(2,1)S(1)} copy-done((bf16[1,1024,768]{2,1,0:T(8,128)(2,1)S(1)}, bf16[1,1024,768]{2,1,0:T(8,128)(2,1)}, u32[]{:S(2)}) %copy-start.1) | copy-done | bytes 1572888
  2.8 0.0 copy-start.2
  2.8 1.4 %copy-done.2 = bf16[1,768,1024]{2,1,0:T(8,128)(2,1)S(1)} copy-done((bf16[1,768,1024]{2,1,0:T(8,128)(2,1)S(1)}, bf16[1,768,1024]{2,1,0:T(8,128)(2,1)}, u32[]{:S(2)}) %copy-start.2) | copy-done | bytes 1572888
  4.2 0.0 copy-start.3
  4.2 0.7 copy-done.3
  4.9 0.0 copy-start.4
  4.9 0.7 copy-done.4
  5.6 0.0 copy-start.5
  5.6 0.7 copy-done.5
  6.3 0.0 copy-start.6
  6.3 0.7 copy-done.6
  7.0 0.0 copy-start.7
  7.0 0.7 copy-done.7
  7.7 0.0 copy-start.8
  7.7 0.7 copy-done.8
  8.3 75.9 %shard_map.91 = bf16[4,1024]{1,0:T(4,128)(2,1)S(1)} custom-call(bf16[4,1024]{1,0:T(4,128)(2,1)S(1)} %copy-done.3, s32[4,8]{1,0:T(4,128)S(1)} %copy-done.4, s32[4,8]{1,0:T(4,128)S(1)} %copy-done.5, bf16[1,1024,768]{2,1,0:T(8,128)(2,1)S(1)} %copy-done, bf16[1,1024,768]{2,1,0:T(8,128)(2,1)S(1)} %copy-done.1, bf16[1,768,1024]{2,1,0:T(8,128)(2,1)S(1)} %copy-done.2, ...), custom_call_target="tpu_custom_call" | custom-call | tf_op jit(solution)/shard_map/pallas_call | solution.py:437
  84.2 0.6 copy.11
Async XLA Ops:
  0.0 1.4 %copy-start = (bf16[1,1024,768]{2,1,0:T(8,128)(2,1)S(1)}, bf16[1,1024,768]{2,1,0:T(8,128)(2,1)}, u32[]{:S(2)}) copy-start(bf16[1,1024,768]{2,1,0:T(8,128)(2,1)} %gate_hbm.1) | copy-start | bytes 4718596
  1.4 1.4 %copy-start.1 = (bf16[1,1024,768]{2,1,0:T(8,128)(2,1)S(1)}, bf16[1,1024,768]{2,1,0:T(8,128)(2,1)}, u32[]{:S(2)}) copy-start(bf16[1,1024,768]{2,1,0:T(8,128)(2,1)} %up_hbm.1) | copy-start | bytes 4718596
  2.8 1.4 %copy-start.2 = (bf16[1,768,1024]{2,1,0:T(8,128)(2,1)S(1)}, bf16[1,768,1024]{2,1,0:T(8,128)(2,1)}, u32[]{:S(2)}) copy-start(bf16[1,768,1024]{2,1,0:T(8,128)(2,1)} %down_hbm.1) | copy-start | bytes 4718596
  4.2 0.7 copy-start.3
  4.9 0.7 copy-start.4
  5.6 0.7 copy-start.5
  6.3 0.7 copy-start.6
  7.0 0.7 copy-start.7
  7.7 0.7 copy-start.8

commit v2 on v1

--- a/solution.py
+++ b/solution.py
@@ -10,7 +10,7 @@
 QB = 128
 CAP = 2
 NX = 4
-CHUNKS = 4
+CHUNKS = 2
 F32 = jnp.float32
 BF16 = jnp.bfloat16
 
@@ -178,7 +178,8 @@
         slots[e : e + 8] = wide[e * 16 : (e + 8) * 16, :].reshape(8, 16, 128).astype(BF16)
 
     c = Copies()
-    pl.semaphore_wait(barrier, 2 * (nz - 1) + 5)
+    with jax.named_scope("greet"):
+        pl.semaphore_wait(barrier, 2 * (nz - 1) + 5)
 
     gathered[h, 0, core] = slots[s]
     c.start(slots.at[z * 2 + 1 - core], gathered.at[h, 0, core], zs.at[1 - core], zr.at[core], chip(0, 1 - core))
@@ -194,8 +195,9 @@
                 dev,
             )
 
-    for load in loads[3:]:
-        load.wait()
+    with jax.named_scope("loads"):
+        for load in loads[3:]:
+            load.wait()
 
     def grow(scale, count):
         v = scale[0].astype(F32)
@@ -220,8 +222,9 @@
         w2[at, :] = (w2[at, :].astype(F32) * grown2[pl.ds(n // 4, 1), :]).astype(BF16)
         return 0
 
-    lax.fori_loop(0, w1.shape[0] // 32, scale_w1, 0)
-    lax.fori_loop(0, w2.shape[0] // 32, scale_w2, 0)
+    with jax.named_scope("scale"):
+        lax.fori_loop(0, w1.shape[0] // 32, scale_w1, 0)
+        lax.fori_loop(0, w2.shape[0] // 32, scale_w2, 0)
 
     def span(k, part=None):
         if part is None:
@@ -362,13 +365,15 @@
     for t in range(len(stages) + nc - 1):
         for k in range(nc):
             if 0 <= t - k < len(stages):
-                stages[t - k](k)
-
-    for i, frm in peers:
-        if i == 0:
-            continue
-        recv(results.at[chip(i, frm)[0]], br.at[i * 2 + frm])
-    recv(results.at[z * 2 + 1 - core], br.at[1 - core])
+                with jax.named_scope(f"s{t - k}c{k}"):
+                    stages[t - k](k)
+
+    with jax.named_scope("back"):
+        for i, frm in peers:
+            if i == 0:
+                continue
+            recv(results.at[chip(i, frm)[0]], br.at[i * 2 + frm])
+        recv(results.at[z * 2 + 1 - core], br.at[1 - core])
 
     high = combine.astype(BF16).astype(F32)
     both = jnp.concatenate([high, combine - high], axis=0)[:, : ne * CAP].astype(BF16)
@@ -437,11 +442,11 @@
         return pl.pallas_call(
             functools.partial(kernel, nz),
             out_shape=jax.ShapeDtypeStruct(tokens.shape, BF16),
-            in_specs=[pl.BlockSpec(memory_space=pl.ANY)] * 9,
+            in_specs=[pl.BlockSpec(memory_space=pltpu.HBM)] * 9,
             out_specs=pl.BlockSpec(memory_space=pltpu.VMEM),
             scratch_shapes=scratch,
             compiler_params=pltpu.CompilerParams(
-                collective_id=0, has_side_effects=True, vmem_limit_bytes=40 * 1024 * 1024
+                collective_id=0, has_side_effects=True, vmem_limit_bytes=60 * 1024 * 1024
             ),
         )(*args)
 

time: 85.2 us -> 71.1 us (0.83)
  local copies, waits for them, and re-layouts: 8.92 us -> 1.3 us
  Pallas kernels: 75.9 us -> 69.4 us
    unnamed x19 -> x1, local copies, waits for them, and re-layouts: 8.92 us -> 1.3 us
    pallas_call x1, Pallas kernels: 75.9 us -> 69.4 us  [step(): pl.pallas_call(functools.partial(kernel, nz), out_shape=jax.ShapeDtypeStr...]
where the time goes in v2:
time: 71.1 us; the launch traced here: 70.7 us
  Pallas kernels  69.4 us (98%)
  local copies, waits for them, and re-layouts  1.3 us (2%)
    pallas_call x1, Pallas kernels, step(): pl.pallas_call(functools.partial(kernel, nz), out_shape=jax.ShapeDtypeStr...  69.4 us

profile of v2, /device:TPU:1, one launch (start us, length us, event | category | flops | bytes accessed | tf_op | source)
XLA Modules:
  0.0 70.7 jit_solution(804911706996910109)
XLA Ops:
  0.0 69.4 %shard_map.91 = bf16[4,1024]{1,0:T(4,128)(2,1)} custom-call(bf16[4,1024]{1,0:T(4,128)(2,1)} %tokens_hbm.1, s32[4,8]{1,0:T(4,128)} %routes_hbm.1, s32[4,8]{1,0:T(4,128)} %fixed_hbm.1, bf16[1,1024,768]{2,1,0:T(8,128)(2,1)} %gate_hbm.1, bf16[1,1024,768]{2,1,0:T(8,128)(2,1)} %up_hbm.1, bf16[1,768,1024]{2,1,0:T(8,128)(2,1)} %down_hbm.1, bf16[1,8,6]{2,1,0:T(8,128)(2,1)} %gs_hbm.1, ...), custom_call_target="tpu_custom_call" | custom-call | tf_op jit(solution)/shard_map/pallas_call | solution.py:442
  69.4 1.3 %copy.11 = bf16[4,1024]{1,0:T(4,128)(2,1)} copy(bf16[4,1024]{1,0:T(4,128)(2,1)} %shard_map.91) | data formatting | bytes 16384

commit v3 on v2

--- a/solution.py
+++ b/solution.py
@@ -10,7 +10,8 @@
 QB = 128
 CAP = 2
 NX = 4
-CHUNKS = 2
+CHUNKS = 4
+ORDER = [divmod(n, 10) for n in (0, 1, 2, 10, 3, 11, 12, 20, 13, 21, 22, 30, 23, 31, 32, 40, 33, 41, 42, 43)]
 F32 = jnp.float32
 BF16 = jnp.bfloat16
 
@@ -74,13 +75,9 @@
     wide,
     x_ref,
     partial,
-    relay_y,
-    sums_y,
     arrive_y,
     hidden,
     outs,
-    relay_x,
-    sums_x,
     arrive_x,
     back_wide,
     back,
@@ -118,8 +115,8 @@
 
     xr, xl, xo = near(h, 1), near(h, -1), near(h, 2)
     yr, yl, yo = near(p, 1), near(p, -1), near(p, 2)
-    dev_xr, dev_xl = (s, xr, p), (s, xl, p)
-    dev_yr, dev_yl = (s, h, yr), (s, h, yl)
+    devs_x = [(s, a, p) for a in (xo, xr, xl)]
+    devs_y = [(s, h, a) for a in (yo, yr, yl)]
 
     def chip(i, to_core):
         return (((z + offset(i) + nz) % nz) * 2 + to_core, h, p)
@@ -130,7 +127,7 @@
     for i in range(nz - 1, 0, -1):
         for c in (0, 1):
             pl.semaphore_signal(barrier, inc=1, device_id=chip(i, c), device_id_type=pl.DeviceIdType.MESH)
-    for dev in (chip(0, 1 - core), dev_xr, dev_xl, dev_yr, dev_yl):
+    for dev in (chip(0, 1 - core), *devs_x, *devs_y):
         pl.semaphore_signal(barrier, inc=1, device_id=dev, device_id_type=pl.DeviceIdType.MESH)
 
     loads = [
@@ -179,7 +176,7 @@
 
     c = Copies()
     with jax.named_scope("greet"):
-        pl.semaphore_wait(barrier, 2 * (nz - 1) + 5)
+        pl.semaphore_wait(barrier, 2 * (nz - 1) + 7)
 
     gathered[h, 0, core] = slots[s]
     c.start(slots.at[z * 2 + 1 - core], gathered.at[h, 0, core], zs.at[1 - core], zr.at[core], chip(0, 1 - core))
@@ -226,13 +223,11 @@
         lax.fori_loop(0, w1.shape[0] // 32, scale_w1, 0)
         lax.fori_loop(0, w2.shape[0] // 32, scale_w2, 0)
 
-    def span(k, part=None):
-        if part is None:
-            return pl.ds(k * ni, ni)
-        return pl.ds(k * ni + part * (ni // 2), ni // 2)
-
-    def recv(dst, sem, send=None):
-        c.make(dst, dst, zs.at[0] if send is None else send, sem, dev_xr).wait_recv()
+    def span(k):
+        return pl.ds(k * ni, ni)
+
+    def recv(dst, sem):
+        c.make(dst, dst, zs.at[0], sem, devs_x[0]).wait_recv()
 
     def stage0(k):
         for i in range(k * ni, (k + 1) * ni):
@@ -243,21 +238,13 @@
         if k == 0:
             recv(gathered.at[h, 0, 1 - core], zr.at[1 - core])
         block = gathered.at[h, span(k)]
-        c.start(block, block, gx_s.at[k, 0], gx_r.at[k, 0], dev_xr)
-        c.start(block, block, gx_s.at[k, 1], gx_r.at[k, 1], dev_xl)
+        for n, dev in enumerate(devs_x):
+            c.start(block, block, gx_s.at[k, n], gx_r.at[k, n], dev)
 
     def stage1(k):
-        recv(gathered.at[xl, span(k)], gx_r.at[k, 0])
-        block = gathered.at[xl, span(k, 1)]
-        c.start(block, block, gx_s.at[k, 2], gx_r.at[k, 2], dev_xr)
-        recv(gathered.at[xr, span(k)], gx_r.at[k, 1])
-        block = gathered.at[xr, span(k, 0)]
-        c.start(block, block, gx_s.at[k, 3], gx_r.at[k, 3], dev_xl)
-
-    def stage2(k):
-        recv(gathered.at[xo, span(k, 1)], gx_r.at[k, 2])
-        recv(gathered.at[xo, span(k, 0)], gx_r.at[k, 3])
         per = ni * 2 * 16
+        for n, a in enumerate((xo, xl, xr)):
+            recv(gathered.at[a, span(k)], gx_r.at[k, n])
         for a in range(NX):
             wide[a * per : (a + 1) * per, :] = (
                 gathered[a, k * ni : (k + 1) * ni].astype(F32).reshape(per, 128)
@@ -273,47 +260,36 @@
             partial[k, n // tiles, :, :, at] = part.reshape(NX, share, 256).astype(BF16)
             return 0
 
-        lax.fori_loop(0, 2 * tiles, tile, 0)
-        c.start(partial.at[k, 0, yo], relay_y.at[k, 0], ry_s.at[k, 0], ry_r.at[k, 0], dev_yr)
-        c.start(partial.at[k, 1, yo], relay_y.at[k, 1], ry_s.at[k, 1], ry_r.at[k, 1], dev_yl)
-        c.start(partial.at[k, 1, yr], arrive_y.at[k, 0, 1], ry_s.at[k, 2], ry_r.at[k, 2], dev_yr)
-        c.start(partial.at[k, 0, yl], arrive_y.at[k, 1, 0], ry_s.at[k, 3], ry_r.at[k, 3], dev_yl)
-
-    def stage3(k):
-        recv(relay_y.at[k, 0], ry_r.at[k, 0])
-        sums_y[k, 0] = (partial[k, 0, yr].astype(F32) + relay_y[k, 0].astype(F32)).astype(BF16)
-        c.start(sums_y.at[k, 0], arrive_y.at[k, 0, 0], ry_s.at[k, 4], ry_r.at[k, 4], dev_yr)
-        recv(relay_y.at[k, 1], ry_r.at[k, 1])
-        sums_y[k, 1] = (partial[k, 1, yl].astype(F32) + relay_y[k, 1].astype(F32)).astype(BF16)
-        c.start(sums_y.at[k, 1], arrive_y.at[k, 1, 1], ry_s.at[k, 5], ry_r.at[k, 5], dev_yl)
-
-    def stage4(k):
-        recv(arrive_y.at[k, 0, 1], ry_r.at[k, 2])
-        recv(arrive_y.at[k, 1, 0], ry_r.at[k, 3])
-        recv(arrive_y.at[k, 0, 0], ry_r.at[k, 4])
-        recv(arrive_y.at[k, 1, 1], ry_r.at[k, 5])
-        g, u = [
-            partial[k, n, p].astype(F32) + arrive_y[k, 0, n].astype(F32) + arrive_y[k, 1, n].astype(F32)
-            for n in (0, 1)
-        ]
+        for half in (0, 1):
+            lax.fori_loop(half * tiles, (half + 1) * tiles, tile, 0)
+            for n, (to, dev) in enumerate(zip((yo, yr, yl), devs_y)):
+                c.start(
+                    partial.at[k, half, to],
+                    arrive_y.at[k, n, half],
+                    ry_s.at[k, half * 3 + n],
+                    ry_r.at[k, half * 3 + n],
+                    dev,
+                )
+
+    def total(mine, arrived, k, half):
+        return mine.astype(F32) + (
+            arrived[k, 0, half].astype(F32) + arrived[k, 1, half].astype(F32) + arrived[k, 2, half].astype(F32)
+        )
+
+    def stage2(k):
+        for half in (0, 1):
+            for n in range(3):
+                recv(arrive_y.at[k, n, half], ry_r.at[k, half * 3 + n])
+        g = total(partial[k, 0, p], arrive_y, k, 0)
+        u = total(partial[k, 1, p], arrive_y, k, 1)
         hidden[k, p] = (g / (1.0 + jnp.exp(-g)) * u).astype(BF16)
         block = hidden.at[k, p]
-        c.start(block, block, gy_s.at[k, 0], gy_r.at[k, 0], dev_yr)
-        c.start(block, block, gy_s.at[k, 1], gy_r.at[k, 1], dev_yl)
-
-    left, right = pl.ds(0, f1 // 2), pl.ds(f1 // 2, f1 // 2)
-
-    def stage5(k):
-        recv(hidden.at[k, yl], gy_r.at[k, 0])
-        block = hidden.at[k, yl, :, left]
-        c.start(block, block, gy_s.at[k, 2], gy_r.at[k, 2], dev_yr)
-        recv(hidden.at[k, yr], gy_r.at[k, 1])
-        block = hidden.at[k, yr, :, right]
-        c.start(block, block, gy_s.at[k, 3], gy_r.at[k, 3], dev_yl)
-
-    def stage6(k):
-        recv(hidden.at[k, yo, :, left], gy_r.at[k, 2])
-        recv(hidden.at[k, yo, :, right], gy_r.at[k, 3])
+        for n, dev in enumerate(devs_y):
+            c.start(block, block, gy_s.at[k, n], gy_r.at[k, n], dev)
+
+    def stage3(k):
+        for n, a in enumerate((yo, yl, yr)):
+            recv(hidden.at[k, a], gy_r.at[k, n])
         tiles = dw // 512
 
         def tile(n, _):
@@ -324,27 +300,23 @@
             outs[k, n // tiles, :, :, at] = part.reshape(NX, share, 256).astype(BF16)
             return 0
 
-        lax.fori_loop(0, 2 * tiles, tile, 0)
-        c.start(outs.at[k, 0, xo], relay_x.at[k, 0], rx_s.at[k, 0], rx_r.at[k, 0], dev_xr)
-        c.start(outs.at[k, 1, xo], relay_x.at[k, 1], rx_s.at[k, 1], rx_r.at[k, 1], dev_xl)
-        c.start(outs.at[k, 1, xr], arrive_x.at[k, 0, 1], rx_s.at[k, 2], rx_r.at[k, 2], dev_xr)
-        c.start(outs.at[k, 0, xl], arrive_x.at[k, 1, 0], rx_s.at[k, 3], rx_r.at[k, 3], dev_xl)
-
-    def stage7(k):
-        recv(relay_x.at[k, 0], rx_r.at[k, 0])
-        sums_x[k, 0] = (outs[k, 0, xr].astype(F32) + relay_x[k, 0].astype(F32)).astype(BF16)
-        c.start(sums_x.at[k, 0], arrive_x.at[k, 0, 0], rx_s.at[k, 4], rx_r.at[k, 4], dev_xr)
-        recv(relay_x.at[k, 1], rx_r.at[k, 1])
-        sums_x[k, 1] = (outs[k, 1, xl].astype(F32) + relay_x[k, 1].astype(F32)).astype(BF16)
-        c.start(sums_x.at[k, 1], arrive_x.at[k, 1, 1], rx_s.at[k, 5], rx_r.at[k, 5], dev_xl)
-
-    def stage8(k):
-        recv(arrive_x.at[k, 0, 1], rx_r.at[k, 2])
-        recv(arrive_x.at[k, 1, 0], rx_r.at[k, 3])
-        recv(arrive_x.at[k, 0, 0], rx_r.at[k, 4])
-        recv(arrive_x.at[k, 1, 1], rx_r.at[k, 5])
+        for half in (0, 1):
+            lax.fori_loop(half * tiles, (half + 1) * tiles, tile, 0)
+            for n, (to, dev) in enumerate(zip((xo, xr, xl), devs_x)):
+                c.start(
+                    outs.at[k, half, to],
+                    arrive_x.at[k, n, half],
+                    rx_s.at[k, half * 3 + n],
+                    rx_r.at[k, half * 3 + n],
+                    dev,
+                )
+
+    def stage4(k):
+        for half in (0, 1):
+            for n in range(3):
+                recv(arrive_x.at[k, n, half], rx_r.at[k, half * 3 + n])
         for n in (0, 1):
-            y = outs[k, n, h].astype(F32) + arrive_x[k, 0, n].astype(F32) + arrive_x[k, 1, n].astype(F32)
+            y = total(outs[k, n, h], arrive_x, k, n)
             for j in range(jw // 2):
                 back_wide[pl.ds(n * (jw // 2) + j, share, stride=jw), :] = y[:, j * 128 : (j + 1) * 128]
         back[k] = back_wide[...].reshape(ni, 2, 16, 128).astype(BF16)
@@ -361,12 +333,10 @@
             c.start(back.at[0, 0, 1 - core], results.at[s], bs.at[1 - core], br.at[core], chip(0, 1 - core))
             results[s] = back[0, 0, core]
 
-    stages = [stage0, stage1, stage2, stage3, stage4, stage5, stage6, stage7, stage8]
-    for t in range(len(stages) + nc - 1):
-        for k in range(nc):
-            if 0 <= t - k < len(stages):
-                with jax.named_scope(f"s{t - k}c{k}"):
-                    stages[t - k](k)
+    stages = [stage0, stage1, stage2, stage3, stage4]
+    for n, k in ORDER:
+        with jax.named_scope(f"s{n}c{k}"):
+            stages[n](k)
 
     with jax.named_scope("back"):
         for i, frm in peers:
@@ -414,26 +384,22 @@
             pltpu.VMEM((max(m, ne * CAP) * 8, 128), F32),
             pltpu.VMEM((m, dw), BF16),
             pltpu.VMEM((nc, 2, NX, share, f1), BF16),
-            pltpu.VMEM((nc, 2, share, f1), BF16),
-            pltpu.VMEM((nc, 2, share, f1), BF16),
-            pltpu.VMEM((nc, 2, 2, share, f1), BF16),
+            pltpu.VMEM((nc, 3, 2, share, f1), BF16),
             pltpu.VMEM((nc, NX, share, f1), BF16),
             pltpu.VMEM((nc, 2, NX, share, dw // 2), BF16),
-            pltpu.VMEM((nc, 2, share, dw // 2), BF16),
-            pltpu.VMEM((nc, 2, share, dw // 2), BF16),
-            pltpu.VMEM((nc, 2, 2, share, dw // 2), BF16),
+            pltpu.VMEM((nc, 3, 2, share, dw // 2), BF16),
             pltpu.VMEM((share * 8, 128), F32),
             pltpu.VMEM((nc, ni, 2, 16, 128), BF16),
             pltpu.VMEM((ne, 16, 128), BF16),
             dma((9,)),
             dma((2 * nz,)),
             dma((2 * nz,)),
-            dma((nc, 4)),
-            dma((nc, 4)),
+            dma((nc, 3)),
+            dma((nc, 3)),
             dma((nc, 6)),
             dma((nc, 6)),
-            dma((nc, 4)),
-            dma((nc, 4)),
+            dma((nc, 3)),
+            dma((nc, 3)),
             dma((nc, 6)),
             dma((nc, 6)),
             dma((2 * nz,)),

time: 71.1 us -> 60.6 us (0.85)
  Pallas kernels: 69.4 us -> 59.1 us
    pallas_call x1, Pallas kernels: 69.4 us -> 59.1 us  [step(): pl.pallas_call(functools.partial(kernel, nz), out_shape=jax.ShapeDtypeStr...]
where the time goes in v3:
time: 60.6 us; the launch traced here: 60.4 us
  Pallas kernels  59.1 us (98%)
  local copies, waits for them, and re-layouts  1.3 us (2%)
    pallas_call x1, Pallas kernels, step(): pl.pallas_call(functools.partial(kernel, nz), out_shape=jax.ShapeDtypeStr...  59.1 us
    unnamed x1, local copies, waits for them, and re-layouts  1.3 us

profile of v3, /device:TPU:1, one launch (start us, length us, event | category | flops | bytes accessed | tf_op | source)
XLA Modules:
  0.0 60.4 jit_solution(15224623687934234689)
XLA Ops:
  0.0 59.1 %shard_map.91 = bf16[4,1024]{1,0:T(4,128)(2,1)} custom-call(bf16[4,1024]{1,0:T(4,128)(2,1)} %tokens_hbm.1, s32[4,8]{1,0:T(4,128)} %routes_hbm.1, s32[4,8]{1,0:T(4,128)} %fixed_hbm.1, bf16[1,1024,768]{2,1,0:T(8,128)(2,1)} %gate_hbm.1, bf16[1,1024,768]{2,1,0:T(8,128)(2,1)} %up_hbm.1, bf16[1,768,1024]{2,1,0:T(8,128)(2,1)} %down_hbm.1, bf16[1,8,6]{2,1,0:T(8,128)(2,1)} %gs_hbm.1, ...), custom_call_target="tpu_custom_call" | custom-call | tf_op jit(solution)/shard_map/pallas_call | solution.py:408
  59.1 1.3 %copy.11 = bf16[4,1024]{1,0:T(4,128)(2,1)} copy(bf16[4,1024]{1,0:T(4,128)(2,1)} %shard_map.91) | data formatting | bytes 16384

commit v4 on v3

--- a/solution.py
+++ b/solution.py
@@ -28,24 +28,15 @@
     return other if other < nz else i
 
 
-class Copies:
-    def __init__(self):
-        self.sent = []
-
-    def make(self, src, dst, send, recv, device):
-        return pltpu.make_async_remote_copy(
-            src_ref=src,
-            dst_ref=dst,
-            send_sem=send,
-            recv_sem=recv,
-            device_id=device,
-            device_id_type=pl.DeviceIdType.MESH,
-        )
-
-    def start(self, *args):
-        copy = self.make(*args)
-        copy.start()
-        self.sent.append(copy)
+def send(src, dst, send_sem, recv_sem, device):
+    pltpu.make_async_remote_copy(
+        src_ref=src,
+        dst_ref=dst,
+        send_sem=send_sem,
+        recv_sem=recv_sem,
+        device_id=device,
+        device_id_type=pl.DeviceIdType.MESH,
+    ).start()
 
 
 def kernel(
@@ -99,8 +90,8 @@
     s = lax.axis_index("seq")
     h = lax.axis_index("head")
     p = lax.axis_index("pool")
-    z = s // 2
-    core = s % 2
+    z = lax.div(s, 2)
+    core = lax.rem(s, 2)
     nc = CHUNKS
     ni = nz // nc
     ne = 2 * nz
@@ -111,7 +102,7 @@
     jw = dw // 128
 
     def near(base, step):
-        return (base + step + NX) % NX
+        return lax.rem(base + (step + NX), NX)
 
     xr, xl, xo = near(h, 1), near(h, -1), near(h, 2)
     yr, yl, yo = near(p, 1), near(p, -1), near(p, 2)
@@ -119,9 +110,7 @@
     devs_y = [(s, h, a) for a in (yo, yr, yl)]
 
     def chip(i, to_core):
-        return (((z + offset(i) + nz) % nz) * 2 + to_core, h, p)
-
-    peers = [(i, c) for i in range(nz) for c in (0, 1)]
+        return (lax.rem(z + (offset(i) + nz), nz) * 2 + to_core, h, p)
 
     barrier = pltpu.get_barrier_semaphore()
     for i in range(nz - 1, 0, -1):
@@ -174,21 +163,20 @@
     for e in range(0, ne, 8):
         slots[e : e + 8] = wide[e * 16 : (e + 8) * 16, :].reshape(8, 16, 128).astype(BF16)
 
-    c = Copies()
     with jax.named_scope("greet"):
         pl.semaphore_wait(barrier, 2 * (nz - 1) + 7)
 
     gathered[h, 0, core] = slots[s]
-    c.start(slots.at[z * 2 + 1 - core], gathered.at[h, 0, core], zs.at[1 - core], zr.at[core], chip(0, 1 - core))
+    send(slots.at[z * 2 + 1 - core], gathered.at[h, 0, core], zs.at[0], zr.at[0], chip(0, 1 - core))
     for i in range(1, nz):
         there = opposite(i, nz)
         for to in (0, 1):
             dev = chip(i, to)
-            c.start(
+            send(
                 slots.at[dev[0]],
                 gathered.at[h, there, core],
-                zs.at[i * 2 + to],
-                zr.at[there * 2 + core],
+                zs.at[0],
+                zr.at[there // ni],
                 dev,
             )
 
@@ -226,48 +214,33 @@
     def span(k):
         return pl.ds(k * ni, ni)
 
-    def recv(dst, sem):
-        c.make(dst, dst, zs.at[0], sem, devs_x[0]).wait_recv()
+    def take(size, sem):
+        pltpu.make_async_copy(size, size, sem).wait()
 
     def stage0(k):
-        for i in range(k * ni, (k + 1) * ni):
-            for frm in (0, 1):
-                if i == 0:
-                    continue
-                recv(gathered.at[h, i, frm], zr.at[i * 2 + frm])
-        if k == 0:
-            recv(gathered.at[h, 0, 1 - core], zr.at[1 - core])
+        take(slots.at[pl.ds(0, 2 * ni - (k == 0))], zr.at[k])
         block = gathered.at[h, span(k)]
         for n, dev in enumerate(devs_x):
-            c.start(block, block, gx_s.at[k, n], gx_r.at[k, n], dev)
+            send(block, block, gx_s.at[0], gx_r.at[k], dev)
 
     def stage1(k):
         per = ni * 2 * 16
-        for n, a in enumerate((xo, xl, xr)):
-            recv(gathered.at[a, span(k)], gx_r.at[k, n])
+        take(gathered.at[pl.ds(0, 3), span(k)], gx_r.at[k])
         for a in range(NX):
             wide[a * per : (a + 1) * per, :] = (
                 gathered[a, k * ni : (k + 1) * ni].astype(F32).reshape(per, 128)
             )
         for j in range(jw):
             x_ref[:, j * 128 : (j + 1) * 128] = wide[pl.ds(j, m, stride=jw), :].astype(BF16)
-        tiles = f1 // 256
-
-        def tile(n, _):
-            cols = pl.ds(pl.multiple_of(n * 256, 256), 256)
-            part = jnp.dot(x_ref[...], w1[:, cols], preferred_element_type=F32)
-            at = pl.ds(pl.multiple_of((n % tiles) * 256, 256), 256)
-            partial[k, n // tiles, :, :, at] = part.reshape(NX, share, 256).astype(BF16)
-            return 0
-
         for half in (0, 1):
-            lax.fori_loop(half * tiles, (half + 1) * tiles, tile, 0)
+            part = jnp.dot(x_ref[...], w1[:, half * f1 : (half + 1) * f1], preferred_element_type=F32)
+            partial[k, half] = part.reshape(NX, share, f1).astype(BF16)
             for n, (to, dev) in enumerate(zip((yo, yr, yl), devs_y)):
-                c.start(
+                send(
                     partial.at[k, half, to],
                     arrive_y.at[k, n, half],
-                    ry_s.at[k, half * 3 + n],
-                    ry_r.at[k, half * 3 + n],
+                    ry_s.at[0],
+                    ry_r.at[k],
                     dev,
                 )
 
@@ -277,44 +250,31 @@
         )
 
     def stage2(k):
-        for half in (0, 1):
-            for n in range(3):
-                recv(arrive_y.at[k, n, half], ry_r.at[k, half * 3 + n])
+        take(arrive_y.at[k], ry_r.at[k])
         g = total(partial[k, 0, p], arrive_y, k, 0)
         u = total(partial[k, 1, p], arrive_y, k, 1)
         hidden[k, p] = (g / (1.0 + jnp.exp(-g)) * u).astype(BF16)
         block = hidden.at[k, p]
         for n, dev in enumerate(devs_y):
-            c.start(block, block, gy_s.at[k, n], gy_r.at[k, n], dev)
+            send(block, block, gy_s.at[0], gy_r.at[k], dev)
 
     def stage3(k):
-        for n, a in enumerate((yo, yl, yr)):
-            recv(hidden.at[k, a], gy_r.at[k, n])
-        tiles = dw // 512
-
-        def tile(n, _):
-            cols = pl.ds(pl.multiple_of(n * 256, 256), 256)
+        take(hidden.at[k, pl.ds(0, 3)], gy_r.at[k])
+        for half in (0, 1):
             act = hidden[k].reshape(m, f1)
-            part = jnp.dot(act, w2[:, cols], preferred_element_type=F32)
-            at = pl.ds(pl.multiple_of((n % tiles) * 256, 256), 256)
-            outs[k, n // tiles, :, :, at] = part.reshape(NX, share, 256).astype(BF16)
-            return 0
-
-        for half in (0, 1):
-            lax.fori_loop(half * tiles, (half + 1) * tiles, tile, 0)
+            part = jnp.dot(act, w2[:, half * dw // 2 : (half + 1) * dw // 2], preferred_element_type=F32)
+            outs[k, half] = part.reshape(NX, share, dw // 2).astype(BF16)
             for n, (to, dev) in enumerate(zip((xo, xr, xl), devs_x)):
-                c.start(
+                send(
                     outs.at[k, half, to],
                     arrive_x.at[k, n, half],
-                    rx_s.at[k, half * 3 + n],
-                    rx_r.at[k, half * 3 + n],
+                    rx_s.at[0],
+                    rx_r.at[k],
                     dev,
                 )
 
     def stage4(k):
-        for half in (0, 1):
-            for n in range(3):
-                recv(arrive_x.at[k, n, half], rx_r.at[k, half * 3 + n])
+        take(arrive_x.at[k], rx_r.at[k])
         for n in (0, 1):
             y = total(outs[k, n, h], arrive_x, k, n)
             for j in range(jw // 2):
@@ -326,11 +286,15 @@
                 if i == 0:
                     continue
                 there = opposite(i, nz)
-                c.start(
-                    back.at[k, n, to], results.at[s], bs.at[i * 2 + to], br.at[there * 2 + core], chip(i, to)
+                send(
+                    back.at[k, n, to],
+                    results.at[s],
+                    bs.at[0],
+                    br.at[there // (nz - ni)],
+                    chip(i, to),
                 )
         if k == 0:
-            c.start(back.at[0, 0, 1 - core], results.at[s], bs.at[1 - core], br.at[core], chip(0, 1 - core))
+            send(back.at[0, 0, 1 - core], results.at[s], bs.at[0], br.at[0], chip(0, 1 - core))
             results[s] = back[0, 0, core]
 
     stages = [stage0, stage1, stage2, stage3, stage4]
@@ -338,23 +302,34 @@
         with jax.named_scope(f"s{n}c{k}"):
             stages[n](k)
 
+    with jax.named_scope("drain"):
+        take(slots.at[pl.ds(0, ne - 1)], zs.at[0])
+        take(gathered.at[pl.ds(0, 3)], gx_s.at[0])
+        take(arrive_y, ry_s.at[0])
+        take(hidden.at[:, pl.ds(0, 3)], gy_s.at[0])
+        take(arrive_x, rx_s.at[0])
+
+    def widen(i):
+        at = chip(i, 0)[0]
+        rows_ = pl.ds(pl.multiple_of(at * 16, 32), 32)
+        wide[rows_, :] = results[pl.ds(at, 2)].astype(F32).reshape(32, 128)
+
+    far = 2 * ni
     with jax.named_scope("back"):
-        for i, frm in peers:
-            if i == 0:
-                continue
-            recv(results.at[chip(i, frm)[0]], br.at[i * 2 + frm])
-        recv(results.at[z * 2 + 1 - core], br.at[1 - core])
+        take(results.at[pl.ds(0, ne - 1 - far)], br.at[0])
+        for i in range(nz - ni):
+            widen(i)
+        take(slots.at[pl.ds(0, ne - 1)], bs.at[0])
+        take(results.at[pl.ds(0, far)], br.at[1])
+        for i in range(nz - ni, nz):
+            widen(i)
 
     high = combine.astype(BF16).astype(F32)
     both = jnp.concatenate([high, combine - high], axis=0)[:, : ne * CAP].astype(BF16)
-    for e in range(0, ne, 8):
-        wide[e * 16 : (e + 8) * 16, :] = results[e : e + 8].astype(F32).reshape(128, 128)
     for j in range(jw):
-        got = wide[pl.ds(j, ne * CAP, stride=jw), :].astype(BF16)
-        part = jnp.dot(both, got, preferred_element_type=F32)
-        out_ref[:, j * 128 : (j + 1) * 128] = (part[:4] + part[4:]).astype(BF16)
-    for copy in c.sent:
-        copy.wait_send()
+        x_ref[: ne * CAP, j * 128 : (j + 1) * 128] = wide[pl.ds(j, ne * CAP, stride=jw), :].astype(BF16)
+    part = jnp.dot(both, x_ref[: ne * CAP], preferred_element_type=F32)
+    out_ref[...] = (part[:4] + part[4:]).astype(BF16)
 
 
 def solution(mesh):
@@ -392,18 +367,18 @@
             pltpu.VMEM((nc, ni, 2, 16, 128), BF16),
             pltpu.VMEM((ne, 16, 128), BF16),
             dma((9,)),
-            dma((2 * nz,)),
-            dma((2 * nz,)),
-            dma((nc, 3)),
-            dma((nc, 3)),
-            dma((nc, 6)),
-            dma((nc, 6)),
-            dma((nc, 3)),
-            dma((nc, 3)),
-            dma((nc, 6)),
-            dma((nc, 6)),
-            dma((2 * nz,)),
-            dma((2 * nz,)),
+            dma((1,)),
+            dma((nc,)),
+            dma((1,)),
+            dma((nc,)),
+            dma((1,)),
+            dma((nc,)),
+            dma((1,)),
+            dma((nc,)),
+            dma((1,)),
+            dma((nc,)),
+            dma((1,)),
+            dma((2,)),
         ]
         return pl.pallas_call(
             functools.partial(kernel, nz),

time: 60.6 us -> 58.2 us (0.960)
  Pallas kernels: 59.1 us -> 56.7 us
    pallas_call x1, Pallas kernels: 59.1 us -> 56.7 us  [step(): pl.pallas_call(functools.partial(kernel, nz), out_shape=jax.ShapeDtypeStr...]
where the time goes in v4:
time: 58.2 us; the launch traced here: 58 us
  Pallas kernels  56.7 us (97%)
  local copies, waits for them, and re-layouts  1.3 us (2%)
    pallas_call x1, Pallas kernels, step(): pl.pallas_call(functools.partial(kernel, nz), out_shape=jax.ShapeDtypeStr...  56.7 us
    unnamed x1, local copies, waits for them, and re-layouts  1.3 us

profile of v4, /device:TPU:1, one launch (start us, length us, event | category | flops | bytes accessed | tf_op | source)
XLA Modules:
  0.0 58.0 jit_solution(18065367742772663505)
XLA Ops:
  0.0 56.7 %shard_map.91 = bf16[4,1024]{1,0:T(4,128)(2,1)} custom-call(bf16[4,1024]{1,0:T(4,128)(2,1)} %tokens_hbm.1, s32[4,8]{1,0:T(4,128)} %routes_hbm.1, s32[4,8]{1,0:T(4,128)} %fixed_hbm.1, bf16[1,1024,768]{2,1,0:T(8,128)(2,1)} %gate_hbm.1, bf16[1,1024,768]{2,1,0:T(8,128)(2,1)} %up_hbm.1, bf16[1,768,1024]{2,1,0:T(8,128)(2,1)} %down_hbm.1, bf16[1,8,6]{2,1,0:T(8,128)(2,1)} %gs_hbm.1, ...), custom_call_target="tpu_custom_call" | custom-call | tf_op jit(solution)/shard_map/pallas_call | solution.py:383
  56.7 1.3 %copy.11 = bf16[4,1024]{1,0:T(4,128)(2,1)} copy(bf16[4,1024]{1,0:T(4,128)(2,1)} %shard_map.91) | data formatting | bytes 16384

commit v5 on v4

--- a/solution.py
+++ b/solution.py
@@ -11,7 +11,7 @@
 CAP = 2
 NX = 4
 CHUNKS = 4
-ORDER = [divmod(n, 10) for n in (0, 1, 2, 10, 3, 11, 12, 20, 13, 21, 22, 30, 23, 31, 32, 40, 33, 41, 42, 43)]
+ORDER = [divmod(n, 10) for n in (3, 2, 1, 0, 13, 12, 11, 23, 10, 22, 21, 33, 20, 32, 31, 43, 30, 42, 41, 40)]
 F32 = jnp.float32
 BF16 = jnp.bfloat16
 
@@ -168,7 +168,7 @@
 
     gathered[h, 0, core] = slots[s]
     send(slots.at[z * 2 + 1 - core], gathered.at[h, 0, core], zs.at[0], zr.at[0], chip(0, 1 - core))
-    for i in range(1, nz):
+    for i in range(nz - 1, 0, -1):
         there = opposite(i, nz)
         for to in (0, 1):
             dev = chip(i, to)

time: 58.2 us -> 57.5 us (0.988)
  Pallas kernels: 56.7 us -> 56 us
    pallas_call x1, Pallas kernels: 56.7 us -> 56 us  [step(): pl.pallas_call(functools.partial(kernel, nz), out_shape=jax.ShapeDtypeStr...]
where the time goes in v5:
time: 57.5 us; the launch traced here: 57.3 us
  Pallas kernels  56 us (97%)
  local copies, waits for them, and re-layouts  1.3 us (2%)
    pallas_call x1, Pallas kernels, step(): pl.pallas_call(functools.partial(kernel, nz), out_shape=jax.ShapeDtypeStr...  56 us
    unnamed x1, local copies, waits for them, and re-layouts  1.3 us

profile of v5, /device:TPU:1, one launch (start us, length us, event | category | flops | bytes accessed | tf_op | source)
XLA Modules:
  0.0 57.3 jit_solution(12075695377737530399)
XLA Ops:
  0.0 56.0 %shard_map.91 = bf16[4,1024]{1,0:T(4,128)(2,1)} custom-call(bf16[4,1024]{1,0:T(4,128)(2,1)} %tokens_hbm.1, s32[4,8]{1,0:T(4,128)} %routes_hbm.1, s32[4,8]{1,0:T(4,128)} %fixed_hbm.1, bf16[1,1024,768]{2,1,0:T(8,128)(2,1)} %gate_hbm.1, bf16[1,1024,768]{2,1,0:T(8,128)(2,1)} %up_hbm.1, bf16[1,768,1024]{2,1,0:T(8,128)(2,1)} %down_hbm.1, bf16[1,8,6]{2,1,0:T(8,128)(2,1)} %gs_hbm.1, ...), custom_call_target="tpu_custom_call" | custom-call | tf_op jit(solution)/shard_map/pallas_call | solution.py:383
  56.0 1.3 %copy.11 = bf16[4,1024]{1,0:T(4,128)(2,1)} copy(bf16[4,1024]{1,0:T(4,128)(2,1)} %shard_map.91) | data formatting | bytes 16384
